TPU v7x, 32 devices: a whole 2x2x4 slice. The times are simulated.
32 devices in a mesh: groups: 2 (over y), row: 4 (over z), col: 2 (over x), sub: 2 (over core).
Axes of the slice: x: 2, y: 2, z: 4, core: 2. Of those that a mesh axis runs over, the one named last changes fastest.
Arguments:
- matrix: float32 [16384, 8192], P(('groups', 'row'), ('col', 'sub')), parts along dimension 0, may hold values from -60 to 60
- basis_vectors: float32 [16384, 1024], P(('groups', 'row'), ('col', 'sub')), parts along dimension 0, may hold values from -0.0625 to 0.0625
- split_size: int32 [2], P('groups'), parts along dimension 0, may hold values from 256 to 767
Outputs:
- children: float32 [2, 2048, 1024], P('sub', ('groups', 'row'), 'col'), parts along dimension 1
There are 2 independent parts, one for each index of `groups`. A program takes and returns all parts, laid end to end along the dimension named above; each array names one. Nothing has to cross between parts.
Inputs may be any that keep to these rules, and one draw needn't show every extreme that they name: The second subspace has 1024 minus split_size vectors.
All inputs are finite; a program needn't handle non-finite values.
Results may differ from a plain program's by a relative error of at most 0.00011.
Values sent between devices are 32-bit elements; how exact they have to be, the bound alone decides.
A program may use at most 128 MiB of HBM per device.

v0:
```python
import jax
import jax.numpy as jnp
from jax import lax
from jax.sharding import PartitionSpec as P


def shards(matrix, basis_vectors, split_size):
    R = lax.axis_size("row")
    S = lax.axis_size("sub")
    C = lax.axis_size("col") * S
    m, kd = basis_vectors.shape
    K = kd * C
    n = matrix.shape[1]
    per = n // m
    piece = m // R
    spread = lax.all_to_all(basis_vectors, "row", split_axis=0, concat_axis=0, tiled=True)
    mine = lax.all_to_all(spread, ("col", "sub"), split_axis=0, concat_axis=1, tiled=True)
    own = lax.all_gather(basis_vectors, ("col", "sub"), axis=1, tiled=True)
    part = lax.dot_general(
        matrix,
        own,
        (((0,), (0,)), ((), ())),
        precision=lax.Precision.HIGH,
        preferred_element_type=jnp.float32,
    )
    part = part.reshape(per, R, piece, K).transpose(1, 0, 2, 3).reshape(R * per * piece, K)
    image = lax.psum_scatter(part, "row", scatter_dimension=0, tiled=True)
    partial_proj = lax.dot_general(
        mine,
        image,
        (((0,), (0,)), ((), ())),
        precision=lax.Precision.HIGH,
        preferred_element_type=jnp.float32,
    )
    proj = lax.psum_scatter(partial_proj, "row", scatter_dimension=0, tiled=True)
    proj = lax.psum_scatter(proj, ("col", "sub"), scatter_dimension=1, tiled=True)
    child_block = lax.all_gather(proj, "sub", axis=1, tiled=True)
    row_ids = (
        jnp.arange(child_block.shape[0], dtype=jnp.int32)
        + lax.axis_index("row") * child_block.shape[0]
    )
    col_ids = (
        jnp.arange(child_block.shape[1], dtype=jnp.int32)
        + lax.axis_index("col") * child_block.shape[1]
    )
    leading = split_size[0]
    row_first = row_ids < leading
    col_first = col_ids < leading
    mask_one = row_first[:, None] & col_first[None, :]
    mask_two = jnp.logical_not(row_first)[:, None] & jnp.logical_not(col_first)[None, :]
    selected = jnp.where(lax.axis_index("sub") == 0, mask_one, mask_two)
    return jnp.where(selected, child_block, jnp.zeros((), jnp.float32))[None]


def solution(mesh):
    placed = (
        P(("groups", "row"), ("col", "sub")),
        P(("groups", "row"), ("col", "sub")),
        P("groups"),
    )
    return jax.shard_map(
        shards,
        mesh=mesh,
        in_specs=placed,
        out_specs=P("sub", ("groups", "row"), "col"),
        check_vma=False,
    )
```

profile of v0, /device:TPU:0, one launch (start us, length us, event | category | flops | bytes accessed | tf_op | source)
XLA Modules:
  0.0 417.1 jit_solution(6435462178155145965)
XLA Ops:
  6.5 0.0 all-gather.2.cloned.1.call-start
  6.5 0.7 all-gather.2.cloned.1.call-update
  7.3 0.0 reduce-scatter.4.cloned.1.call-start
  7.3 62.6 %all-gather.2.cloned.1.call-done = f32[2048,1024]{1,0:T(8,128)} async-done(((f32[2048,256]{1,0:T(8,128)}), f32[2048,1024]{1,0:T(8,128)}) %all-gather.2.cloned.1.call-update) | async-done | bytes 8388624 | tf_op jit(solution)/shard_map/all_gather | solution.py:18
  69.9 33.4 %fusion.2 = f32[2048,1024]{1,0:T(8,128)} fusion(f32[2048,2048]{1,0:T(8,128)} %param.3, f32[2048,1024]{1,0:T(8,128)} %all-gather.2.cloned.1.call-done), kind=kOutput, calls=%fused_computation.6 | convolution fusion | flops 25769803776 | bytes 33554432 | tf_op jit(solution)/shard_map/dot_general | solution.py:19
  103.3 0.0 copy-start
  103.3 0.0 reduce-scatter.4.cloned.1.call-update
  103.4 0.0 reduce-scatter.6.cloned.1.call-start
  103.4 1.5 copy-done
  104.9 109.4 %all_to_all.25 = f32[4,512,256]{2,1,0:T(8,128)S(1)} all-to-all(f32[4,512,256]{2,1,0:T(8,128)S(1)} %bitcast.14), channel_id=1, replica_groups=mesh['groups'=2,'row'=4,'col'=2,'sub'=2] {'row'}, dimensions={0} | all-to-all | bytes 4194304 | tf_op jit(solution)/shard_map/all_to_all | solution.py:16
  214.3 28.1 %all_to_all.26 = f32[4,512,256]{2,1,0:T(8,128)S(1)} all-to-all(f32[4,512,256]{2,1,0:T(8,128)S(1)} %all_to_all.25), channel_id=1, replica_groups=mesh['groups'=2,'row'=4,'col'=2,'sub'=2] {'col','sub'}, dimensions={0} | all-to-all | bytes 4194304 | tf_op jit(solution)/shard_map/all_to_all | solution.py:17
  242.4 1.8 copy.6
  244.3 42.5 %reduce-scatter.4.cloned.1.call-done = f32[512,1024]{1,0:T(8,128)} async-done(((f32[2048,1024]{1,0:T(8,128)}), f32[512,1024]{1,0:T(8,128)}) %reduce-scatter.4.cloned.1.call-update) | async-done | bytes 2097168 | tf_op jit(solution)/shard_map/reduce_scatter | solution.py:27
  286.8 10.8 %convolution_bitcast_fusion = f32[1024,1024]{0,1:T(8,128)} fusion(f32[512,1024]{1,0:T(8,128)} %reduce-scatter.4.cloned.1.call-done, f32[512,1024]{0,1:T(8,128)} %bitcast.16), kind=kOutput, calls=%fused_computation | convolution fusion | flops 3221225472 | bytes 8388608 | tf_op jit(solution)/shard_map/dot_general | solution.py:28
  297.6 0.0 reduce-scatter.6.cloned.1.call-update
  297.6 0.0 reduce-scatter.8.cloned.1.call-start
  297.7 81.6 %reduce-scatter.6.cloned.1.call-done = f32[256,1024]{0,1:T(8,128)} async-done(((f32[1024,1024]{0,1:T(8,128)}), f32[256,1024]{0,1:T(8,128)}) %reduce-scatter.6.cloned.1.call-update) | async-done | bytes 1048592 | tf_op jit(solution)/shard_map/reduce_scatter | solution.py:35
  379.3 0.0 reduce-scatter.8.cloned.1.call-update
  380.0 27.0 %reduce-scatter.8.cloned.1.call-done = f32[256,256]{0,1:T(8,128)} async-done(((f32[256,1024]{0,1:T(8,128)}), f32[256,256]{0,1:T(8,128)}) %reduce-scatter.8.cloned.1.call-update) | async-done | bytes 262160 | tf_op jit(solution)/shard_map/reduce_scatter | solution.py:36
  407.0 2.4 all_gather.7
  409.4 0.2 select_bitcast_fusion
  409.6 1.0 copy.7
  (2 shorter events, 0.0 us)
Async XLA Ops:
  6.5 63.4 %all-gather.2.cloned.1.call-start = ((), (), s32[]{:S(2)}) async-start(), calls=%async_computation.5 | async-start | bytes 10485760 | tf_op jit(solution)/shard_map/all_gather | solution.py:18
  7.3 279.5 %reduce-scatter.4.cloned.1.call-start = ((), (), s32[]{:S(2)}) async-start(), calls=%async_computation.6 | async-start | bytes 10485760 | tf_op jit(solution)/shard_map/reduce_scatter | solution.py:27
  103.3 1.6 copy-start
  103.4 275.9 %reduce-scatter.6.cloned.1.call-start = ((), (), s32[]{:S(2)}) async-start(), calls=%async_computation.7 | async-start | bytes 5242880 | tf_op jit(solution)/shard_map/reduce_scatter | solution.py:35
  297.6 109.3 %reduce-scatter.8.cloned.1.call-start = ((), (), s32[]{:S(2)}) async-start(), calls=%async_computation.8 | async-start | bytes 1310720 | tf_op jit(solution)/shard_map/reduce_scatter | solution.py:36
Sparse Core Ops, SparseCore 0:
  8.9 60.9 all-gather.1
  103.5 183.2 reduce-scatter.3
  297.8 81.4 reduce-scatter.5
  381.7 25.2 reduce-scatter.7
where the time goes:
time: 417 us
  waiting for transfers between devices  214 us (51%)
  blocking collectives  140 us (34%)
  matrix products  44.3 us (11%)
  between operations  13.8 us (3%)
  local copies, waits for them, and re-layouts  4.35 us (1%)
    all_to_all x1, blocking collectives, shards(): lax.all_to_all(basis_vectors, 'row', split_axis=0, concat_axis=0, tiled=T...  109 us
    reduce_scatter x1, waiting for transfers between devices, shards(): lax.psum_scatter(partial_proj, 'row', scatter_dimension=0, tiled=True)  81.6 us
    all_gather x1, waiting for transfers between devices, shards(): own = lax.all_gather(basis_vectors, ('col', 'sub'), axis=1, tiled=True)  62.6 us
    reduce_scatter x1, waiting for transfers between devices, shards(): image = lax.psum_scatter(part, 'row', scatter_dimension=0, tiled=True)  42.5 us
    dot_general x1, matrix products, shards(): lax.dot_general(matrix, own, (((0,), (0,)), ((), ())), precision=lax.Prec...  33.4 us
    all_to_all x1, blocking collectives, shards(): lax.all_to_all(spread, ('col', 'sub'), split_axis=0, concat_axis=1, tiled...  28.1 us
    reduce_scatter x1, waiting for transfers between devices, shards(): lax.psum_scatter(proj, ('col', 'sub'), scatter_dimension=1, tiled=True)  27 us
    dot_general x1, matrix products, shards(): lax.dot_general(mine, image, (((0,), (0,)), ((), ())), precision=lax.Prec...  10.8 us
  transfers between devices with their start and end apart: 4, of which 4 were waited for; matrix products, arithmetic and copies ran while one was open for 0% of the time, Pallas kernels for 0%

commit v1 on v0

--- a/solution.py
+++ b/solution.py
@@ -15,7 +15,12 @@
     piece = m // R
     spread = lax.all_to_all(basis_vectors, "row", split_axis=0, concat_axis=0, tiled=True)
     mine = lax.all_to_all(spread, ("col", "sub"), split_axis=0, concat_axis=1, tiled=True)
-    own = lax.all_gather(basis_vectors, ("col", "sub"), axis=1, tiled=True)
+    own = jnp.concatenate(
+        lax.all_to_all(
+            jnp.stack([basis_vectors] * lax.axis_size(("col", "sub"))), ("col", "sub"), 0, 0
+        ),
+        axis=1,
+    )
     part = lax.dot_general(
         matrix,
         own,

time: 417 us -> 479 us (1.15)
  blocking collectives: 140 us -> 237 us
  waiting for transfers between devices: 214 us -> 151 us
  matrix products: 44.3 us -> 69 us
    all_to_all x0 -> x1, blocking collectives: none -> 97.1 us  [shards(): lax.all_to_all(jnp.stack([basis_vectors] * lax.axis_size(('col', 'sub')))...]
    all_gather x1 -> x0, waiting for transfers between devices: 62.6 us -> none  [shards(): own = lax.all_gather(basis_vectors, ('col', 'sub'), axis=1, tiled=True)]
    dot_general x1, matrix products: 33.4 us -> 58.2 us  [shards(): lax.dot_general(matrix, own, (((0,), (0,)), ((), ())), precision=lax.Prec...]
  transfers between devices with their start and end apart: 4 -> 3, of which waited for: 4 -> 3; matrix products, arithmetic and copies ran while one was open for 0% -> 0% of each run, Pallas kernels for 0% -> 0%
where the time goes in v1:
time: 479 us
  blocking collectives  237 us (49%)
  waiting for transfers between devices  151 us (32%)
  matrix products  69 us (14%)
  between operations  13.8 us (3%)
  local copies, waits for them, and re-layouts  7.28 us (2%)
    all_to_all x1, blocking collectives, shards(): lax.all_to_all(basis_vectors, 'row', split_axis=0, concat_axis=0, tiled=T...  109 us
    all_to_all x1, blocking collectives, shards(): lax.all_to_all(jnp.stack([basis_vectors] * lax.axis_size(('col', 'sub')))...  97.1 us
    reduce_scatter x1, waiting for transfers between devices, shards(): lax.psum_scatter(partial_proj, 'row', scatter_dimension=0, tiled=True)  80.9 us
    dot_general x1, matrix products, shards(): lax.dot_general(matrix, own, (((0,), (0,)), ((), ())), precision=lax.Prec...  58.2 us
    reduce_scatter x1, waiting for transfers between devices, shards(): image = lax.psum_scatter(part, 'row', scatter_dimension=0, tiled=True)  43.1 us
    all_to_all x1, blocking collectives, shards(): lax.all_to_all(spread, ('col', 'sub'), split_axis=0, concat_axis=1, tiled...  28.1 us
    reduce_scatter x1, waiting for transfers between devices, shards(): lax.psum_scatter(proj, ('col', 'sub'), scatter_dimension=1, tiled=True)  27.1 us
    dot_general x1, matrix products, shards(): lax.dot_general(mine, image, (((0,), (0,)), ((), ())), precision=lax.Prec...  10.8 us
  transfers between devices with their start and end apart: 3, of which 3 were waited for; matrix products, arithmetic and copies ran while one was open for 0% of the time, Pallas kernels for 0%

profile of v1, /device:TPU:0, one launch (start us, length us, event | category | flops | bytes accessed | tf_op | source)
XLA Modules:
  0.0 478.6 jit_solution(4890574343754657248)
XLA Ops:
  6.5 0.0 reduce-scatter.4.cloned.1.call-start
  6.5 1.9 copy.7
  8.5 1.0 stack.2
  9.5 97.1 %all_to_all.30 = f32[4,2048,256]{1,2,0:T(8,128)S(1)} all-to-all(f32[4,2048,256]{1,2,0:T(8,128)S(1)} %stack.2), channel_id=1, replica_groups=mesh['groups'=2,'row'=4,'col'=2,'sub'=2] {'col','sub'}, dimensions={0} | all-to-all | bytes 16777216 | tf_op jit(solution)/shard_map/all_to_all | solution.py:19
  106.6 58.2 %fusion.2 = f32[2048,1024]{1,0:T(8,128)} fusion(f32[2048,2048]{1,0:T(8,128)} %param.3, f32[2048,1024]{0,1:T(8,128)S(1)} %bitcast.17), kind=kOutput, calls=%fused_computation.6 | convolution fusion | flops 25769803776 | bytes 33554432 | tf_op jit(solution)/shard_map/dot_general | solution.py:24
  164.8 0.0 copy-start
  164.8 0.0 reduce-scatter.4.cloned.1.call-update
  164.8 0.0 reduce-scatter.6.cloned.1.call-start
  164.9 1.5 copy-done
  166.4 109.4 %all_to_all.31 = f32[4,512,256]{2,1,0:T(8,128)S(1)} all-to-all(f32[4,512,256]{2,1,0:T(8,128)S(1)} %bitcast.18), channel_id=1, replica_groups=mesh['groups'=2,'row'=4,'col'=2,'sub'=2] {'row'}, dimensions={0} | all-to-all | bytes 4194304 | tf_op jit(solution)/shard_map/all_to_all | solution.py:16
  275.8 28.1 %all_to_all.32 = f32[4,512,256]{2,1,0:T(8,128)S(1)} all-to-all(f32[4,512,256]{2,1,0:T(8,128)S(1)} %all_to_all.31), channel_id=1, replica_groups=mesh['groups'=2,'row'=4,'col'=2,'sub'=2] {'col','sub'}, dimensions={0} | all-to-all | bytes 4194304 | tf_op jit(solution)/shard_map/all_to_all | solution.py:17
  303.9 1.8 copy.8
  305.8 43.1 %reduce-scatter.4.cloned.1.call-done = f32[512,1024]{1,0:T(8,128)} async-done(((f32[2048,1024]{1,0:T(8,128)}), f32[512,1024]{1,0:T(8,128)}) %reduce-scatter.4.cloned.1.call-update) | async-done | bytes 2097168 | tf_op jit(solution)/shard_map/reduce_scatter | solution.py:32
  348.8 10.8 %convolution_bitcast_fusion = f32[1024,1024]{0,1:T(8,128)} fusion(f32[512,1024]{1,0:T(8,128)} %reduce-scatter.4.cloned.1.call-done, f32[512,1024]{0,1:T(8,128)} %bitcast.20), kind=kOutput, calls=%fused_computation | convolution fusion | flops 3221225472 | bytes 8388608 | tf_op jit(solution)/shard_map/dot_general | solution.py:33
  359.7 0.0 reduce-scatter.6.cloned.1.call-update
  359.7 0.0 reduce-scatter.8.cloned.1.call-start
  359.7 80.9 %reduce-scatter.6.cloned.1.call-done = f32[256,1024]{0,1:T(8,128)} async-done(((f32[1024,1024]{0,1:T(8,128)}), f32[256,1024]{0,1:T(8,128)}) %reduce-scatter.6.cloned.1.call-update) | async-done | bytes 1048592 | tf_op jit(solution)/shard_map/reduce_scatter | solution.py:40
  440.6 0.0 reduce-scatter.8.cloned.1.call-update
  441.4 27.1 %reduce-scatter.8.cloned.1.call-done = f32[256,256]{0,1:T(8,128)} async-done(((f32[256,1024]{0,1:T(8,128)}), f32[256,256]{0,1:T(8,128)}) %reduce-scatter.8.cloned.1.call-update) | async-done | bytes 262160 | tf_op jit(solution)/shard_map/reduce_scatter | solution.py:41
  468.5 2.4 all_gather.3
  470.9 0.2 select_bitcast_fusion
  471.1 1.0 copy.9
  (2 shorter events, 0.0 us)
Async XLA Ops:
  6.5 342.3 %reduce-scatter.4.cloned.1.call-start = ((), (), s32[]{:S(2)}) async-start(), calls=%async_computation.6 | async-start | bytes 10485760 | tf_op jit(solution)/shard_map/reduce_scatter | solution.py:32
  164.8 1.6 copy-start
  164.8 275.8 %reduce-scatter.6.cloned.1.call-start = ((), (), s32[]{:S(2)}) async-start(), calls=%async_computation.7 | async-start | bytes 5242880 | tf_op jit(solution)/shard_map/reduce_scatter | solution.py:40
  359.7 108.8 %reduce-scatter.8.cloned.1.call-start = ((), (), s32[]{:S(2)}) async-start(), calls=%async_computation.8 | async-start | bytes 1310720 | tf_op jit(solution)/shard_map/reduce_scatter | solution.py:41
Sparse Core Ops, SparseCore 0:
  164.9 183.8 reduce-scatter.3
  359.8 80.7 reduce-scatter.5
  443.2 25.2 reduce-scatter.7
